TPU v7x, 32 devices: a whole 2x2x4 slice. The times are simulated.
32 devices in a mesh: scen: 8 (over z, x), blk: 4 (over y, core).
Axes of the slice: x: 2, y: 2, z: 4, core: 2. Of those that a mesh axis runs over, the one named last changes fastest.
Arguments:
- cons_matrix: bfloat16 [2048, 4096], P(None, 'blk'), may hold values from -0.09375 to 0.09375
- row_scale: float32 [512, 2048], P('scen'), may hold values from 0.5 to 2
- rhs: float32 [512, 2048], P('scen'), may hold values from -6 to 6
- cons_mult: float32 [512, 2048], P('scen'), may hold values from -3 to 3
- cost: float32 [512, 4096], P('scen', 'blk'), may hold values from -6 to 6
- ph_mult: float32 [512, 4096], P('scen', 'blk'), may hold values from -3 to 3
- start: float32 [512, 4096], P('scen', 'blk'), may hold values from -3 to 3
- consensus: float32 [4096], P('blk'), may hold values from -3 to 3
- upper: float32 [4096], P('blk'), may hold values from 0.3 to 1.5
- prob: float32 [512], P('scen'), may hold values from 1 to 30, as said below
Outputs:
- solutions: float32 [512, 4096], P('scen', 'blk')
- mult_new: float32 [512, 2048], P('scen', 'blk')
- z_new: float32 [4096], P('blk')
- w_new: float32 [512, 4096], P('scen', 'blk')
- primal_res: float32 [], replicated
- dual_res: float32 [], replicated
Inputs may be any that keep to these rules, and one draw needn't show every extreme that they name: prob is positive.
All inputs are finite; a program needn't handle non-finite values.
Results may differ from a plain program's by a relative error of at most 0.0017.
Values may be sent and summed in bfloat16 or wider, within the bound.
A program may use at most 64 MiB of HBM per device.

v0:
```python
import jax
import jax.numpy as jnp
from jax import lax
from jax.sharding import PartitionSpec as P

NV = 4096
ITERS = 8


penalty = 1.0
aug_weight = 1.0
step_size = 0.05
eps = 1e-06


def per_device(
    cons_matrix, row_scale, rhs, cons_mult, cost, ph_mult, start, consensus, upper, prob
):
    n_blk = lax.axis_size("blk")
    n_scen = lax.axis_size("scen")
    share_rows = cons_matrix.shape[0] // n_blk
    first_row = lax.axis_index("blk") * share_rows
    own_scale = lax.dynamic_slice_in_dim(row_scale, first_row, share_rows, 1)
    own_rhs = lax.dynamic_slice_in_dim(rhs, first_row, share_rows, 1)
    own_mult = lax.dynamic_slice_in_dim(cons_mult, first_row, share_rows, 1)
    contract = (((1,), (1,)), ((), ()))
    x_now = start
    low_box = -upper[None, :]
    high_box = upper[None, :]
    for step in range(ITERS):
        partial_value = lax.dot_general(
            x_now.astype(jnp.bfloat16), cons_matrix, contract, preferred_element_type=jnp.float32
        )
        prod_share = lax.psum_scatter(partial_value, "blk", scatter_dimension=1, tiled=True)
        weighted_share = (
            own_scale * (own_mult + aug_weight * (own_scale * prod_share - own_rhs))
        ).astype(jnp.bfloat16)
        back = jnp.dot(
            lax.all_gather(weighted_share, "blk", axis=1, tiled=True),
            cons_matrix,
            preferred_element_type=jnp.float32,
        )
        grad = cost + ph_mult + penalty * (x_now - consensus[None, :]) + back
        x_now = jnp.clip(x_now - step_size * grad, low_box, high_box)
    partial_end = lax.dot_general(
        x_now.astype(jnp.bfloat16), cons_matrix, contract, preferred_element_type=jnp.float32
    )
    prod_end = lax.psum_scatter(partial_end, "blk", scatter_dimension=1, tiled=True)
    mult_new = own_mult + aug_weight * (own_scale * prod_end - own_rhs)
    weighted_x = prob[:, None] * x_now
    local_sum = jnp.sum(weighted_x, axis=0)
    local_total = jnp.sum(prob)
    sums, total = lax.psum((local_sum, local_total), "scen")
    z_new = sums / total
    primal_local = jnp.sum(prob[:, None] * (x_now - z_new[None, :]) ** 2)
    dual_local = jnp.sum((z_new - consensus) ** 2) * (1.0 / n_scen)
    primal_sum, dual_sum = lax.psum((primal_local, dual_local), ("scen", "blk"))
    w_new = ph_mult + penalty * (x_now - z_new[None, :])
    primal_res = jnp.sqrt(primal_sum / (total * NV) + eps)
    dual_res = penalty * jnp.sqrt(dual_sum / NV + eps)
    return (x_now, mult_new, z_new, w_new, primal_res, dual_res)


def solution(mesh):
    in_specs = (
        P(None, "blk"),
        P("scen", None),
        P("scen", None),
        P("scen", None),
        P("scen", "blk"),
        P("scen", "blk"),
        P("scen", "blk"),
        P("blk"),
        P("blk"),
        P("scen"),
    )
    out_specs = (P("scen", "blk"), P("scen", "blk"), P("blk"), P("scen", "blk"), P(), P())
    return jax.shard_map(
        per_device, mesh=mesh, in_specs=in_specs, out_specs=out_specs, check_vma=False
    )
```

profile of v0, /device:TPU:0, one launch (start us, length us, event | category | flops | bytes accessed | tf_op | source)
XLA Modules:
  0.0 363.5 jit_solution(18422176172987149110)
XLA Ops:
  7.3 4.6 %fusion.48 = f32[64,2048]{1,0:T(8,128)} fusion(bf16[2048,1024]{1,0:T(8,128)(2,1)} %param.10, f32[64,1024]{1,0:T(8,128)} %param.16), kind=kOutput, calls=%fused_computation.68 | convolution fusion | flops 268500992 | bytes 4980736 | tf_op jit(solution)/shard_map/dot_general | solution.py:31
  12.1 24.4 %reduce-scatter.10.cloned.1.call-done = f32[64,512]{1,0:T(8,128)} async-done(((f32[64,2048]{1,0:T(8,128)}), f32[64,512]{1,0:T(8,128)}) %reduce-scatter.10.cloned.1.call-update) | async-done | bytes 131088 | tf_op jit(solution)/shard_map/reduce_scatter | solution.py:34
  37.6 5.9 %all_gather.24 = bf16[64,2048]{1,0:T(8,128)(2,1)S(1)} all-gather(bf16[64,512]{1,0:T(8,128)(2,1)S(1)} %multiply_convert_fusion.7), channel_id=1, replica_groups=mesh['scen'=8,'blk'=4] {'blk'}, dimensions={1}, use_global_device_ids=true | all-gather | bytes 327680 | tf_op jit(solution)/shard_map/all_gather | solution.py:39
  43.5 3.1 fusion.17
  48.9 21.8 %reduce-scatter.12.cloned.1.call-done = f32[64,512]{1,0:T(8,128)} async-done(((f32[64,2048]{1,0:T(8,128)}), f32[64,512]{1,0:T(8,128)}) %reduce-scatter.12.cloned.1.call-update) | async-done | bytes 131088 | tf_op jit(solution)/shard_map/reduce_scatter | solution.py:34
  71.7 5.9 %all_gather.25 = bf16[64,2048]{1,0:T(8,128)(2,1)S(1)} all-gather(bf16[64,512]{1,0:T(8,128)(2,1)S(1)} %multiply_convert_fusion.6), channel_id=1, replica_groups=mesh['scen'=8,'blk'=4] {'blk'}, dimensions={1}, use_global_device_ids=true | all-gather | bytes 327680 | tf_op jit(solution)/shard_map/all_gather | solution.py:39
  77.6 3.1 fusion.19
  80.8 2.2 fusion.44
  83.0 21.8 %reduce-scatter.14.cloned.1.call-done = f32[64,512]{1,0:T(8,128)} async-done(((f32[64,2048]{1,0:T(8,128)}), f32[64,512]{1,0:T(8,128)}) %reduce-scatter.14.cloned.1.call-update) | async-done | bytes 131088 | tf_op jit(solution)/shard_map/reduce_scatter | solution.py:34
  105.9 5.9 %all_gather.26 = bf16[64,2048]{1,0:T(8,128)(2,1)S(1)} all-gather(bf16[64,512]{1,0:T(8,128)(2,1)S(1)} %multiply_convert_fusion.5), channel_id=1, replica_groups=mesh['scen'=8,'blk'=4] {'blk'}, dimensions={1}, use_global_device_ids=true | all-gather | bytes 327680 | tf_op jit(solution)/shard_map/all_gather | solution.py:39
  111.8 3.1 fusion.21
  117.2 21.8 %reduce-scatter.16.cloned.1.call-done = f32[64,512]{1,0:T(8,128)} async-done(((f32[64,2048]{1,0:T(8,128)}), f32[64,512]{1,0:T(8,128)}) %reduce-scatter.16.cloned.1.call-update) | async-done | bytes 131088 | tf_op jit(solution)/shard_map/reduce_scatter | solution.py:34
  140.0 5.9 %all_gather.27 = bf16[64,2048]{1,0:T(8,128)(2,1)S(1)} all-gather(bf16[64,512]{1,0:T(8,128)(2,1)S(1)} %multiply_convert_fusion.4), channel_id=1, replica_groups=mesh['scen'=8,'blk'=4] {'blk'}, dimensions={1}, use_global_device_ids=true | all-gather | bytes 327680 | tf_op jit(solution)/shard_map/all_gather | solution.py:39
  146.0 3.1 fusion.23
  149.1 2.2 fusion.40
  151.3 21.8 %reduce-scatter.18.cloned.1.call-done = f32[64,512]{1,0:T(8,128)} async-done(((f32[64,2048]{1,0:T(8,128)}), f32[64,512]{1,0:T(8,128)}) %reduce-scatter.18.cloned.1.call-update) | async-done | bytes 131088 | tf_op jit(solution)/shard_map/reduce_scatter | solution.py:34
  174.2 5.9 %all_gather.28 = bf16[64,2048]{1,0:T(8,128)(2,1)S(1)} all-gather(bf16[64,512]{1,0:T(8,128)(2,1)S(1)} %multiply_convert_fusion.3), channel_id=1, replica_groups=mesh['scen'=8,'blk'=4] {'blk'}, dimensions={1}, use_global_device_ids=true | all-gather | bytes 327680 | tf_op jit(solution)/shard_map/all_gather | solution.py:39
  180.1 3.1 fusion.25
  185.7 21.6 %reduce-scatter.20.cloned.1.call-done = f32[64,512]{1,0:T(8,128)} async-done(((f32[64,2048]{1,0:T(8,128)}), f32[64,512]{1,0:T(8,128)}) %reduce-scatter.20.cloned.1.call-update) | async-done | bytes 131088 | tf_op jit(solution)/shard_map/reduce_scatter | solution.py:34
  208.4 5.9 %all_gather.29 = bf16[64,2048]{1,0:T(8,128)(2,1)S(1)} all-gather(bf16[64,512]{1,0:T(8,128)(2,1)S(1)} %multiply_convert_fusion.2), channel_id=1, replica_groups=mesh['scen'=8,'blk'=4] {'blk'}, dimensions={1}, use_global_device_ids=true | all-gather | bytes 327680 | tf_op jit(solution)/shard_map/all_gather | solution.py:39
  214.3 3.1 fusion.27
  217.4 2.2 fusion.36
  219.6 21.8 %reduce-scatter.22.cloned.1.call-done = f32[64,512]{1,0:T(8,128)} async-done(((f32[64,2048]{1,0:T(8,128)}), f32[64,512]{1,0:T(8,128)}) %reduce-scatter.22.cloned.1.call-update) | async-done | bytes 131088 | tf_op jit(solution)/shard_map/reduce_scatter | solution.py:34
  242.5 5.9 %all_gather.30 = bf16[64,2048]{1,0:T(8,128)(2,1)S(1)} all-gather(bf16[64,512]{1,0:T(8,128)(2,1)S(1)} %multiply_convert_fusion.1), channel_id=1, replica_groups=mesh['scen'=8,'blk'=4] {'blk'}, dimensions={1}, use_global_device_ids=true | all-gather | bytes 327680 | tf_op jit(solution)/shard_map/all_gather | solution.py:39
  248.4 3.1 fusion.29
  251.5 2.2 fusion.34
  253.8 21.8 %reduce-scatter.24.cloned.1.call-done = f32[64,512]{1,0:T(8,128)} async-done(((f32[64,2048]{1,0:T(8,128)}), f32[64,512]{1,0:T(8,128)}) %reduce-scatter.24.cloned.1.call-update) | async-done | bytes 131088 | tf_op jit(solution)/shard_map/reduce_scatter | solution.py:34
  276.7 5.9 %all_gather.31 = bf16[64,2048]{1,0:T(8,128)(2,1)S(1)} all-gather(bf16[64,512]{1,0:T(8,128)(2,1)S(1)} %multiply_convert_fusion), channel_id=1, replica_groups=mesh['scen'=8,'blk'=4] {'blk'}, dimensions={1}, use_global_device_ids=true | all-gather | bytes 327680 | tf_op jit(solution)/shard_map/all_gather | solution.py:39
  282.6 3.1 multiply_reduce_fusion.1
  285.7 2.2 fusion.32
  288.5 22.2 %all-reduce.1 = (f32[1024]{0:T(1024)S(1)}, f32[]{:T(128)}) all-reduce(f32[1024]{0:T(1024)S(1)} %get-tuple-element.14, f32[]{:T(128)} %reduce_sum.37), channel_id=1, replica_groups=mesh['scen'=8,'blk'=4] {'scen'}, use_global_device_ids=true, to_apply=%region_10.11 | all-reduce | flops 1025 | bytes 8200 | tf_op jit(solution)/shard_map/psum | solution.py:53
  314.0 37.0 %all-reduce = (f32[]{:T(128)}, f32[]{:T(128)}) all-reduce(f32[]{:T(128)} %get-tuple-element.12, f32[]{:T(128)S(6)} %mul.128), channel_id=1, replica_groups=mesh['scen'=8,'blk'=4] {'scen','blk'}, use_global_device_ids=true, to_apply=%region_14.15 | all-reduce | flops 2 | bytes 16 | tf_op jit(solution)/shard_map/psum | solution.py:57
  (74 shorter events, 21.0 us)
Async XLA Ops:
  7.2 36.3 %copy-start.12 = (f32[64,1024]{1,0:T(8,128)S(1)}, f32[64,1024]{1,0:T(8,128)}, u32[]{:S(2)}) copy-start(f32[64,1024]{1,0:T(8,128)} %param.16) | copy-start | bytes 786436
  7.2 4.8 %copy-start.14 = (f32[1024]{0:T(1024)S(1)}, f32[1024]{0:T(1024)}, u32[]{:S(2)}) copy-start(f32[1024]{0:T(1024)} %param.18) | copy-start | bytes 12292
  7.2 4.8 %copy-start.16 = (f32[64,1024]{1,0:T(8,128)S(1)}, f32[64,1024]{1,0:T(8,128)}, u32[]{:S(2)}) copy-start(f32[64,1024]{1,0:T(8,128)} %param.14) | copy-start | bytes 786436
  7.2 4.8 %copy-start.13 = (f32[64,1024]{1,0:T(8,128)S(1)}, f32[64,1024]{1,0:T(8,128)}, u32[]{:S(2)}) copy-start(f32[64,1024]{1,0:T(8,128)} %param.15) | copy-start | bytes 786436
  7.2 29.2 %copy-start.8 = (f32[64,2048]{1,0:T(8,128)S(1)}, f32[64,2048]{1,0:T(8,128)}, u32[]{:S(2)}) copy-start(f32[64,2048]{1,0:T(8,128)} %param.12) | copy-start | bytes 1572868
  7.2 29.2 %copy-start.9 = (f32[64,2048]{1,0:T(8,128)S(1)}, f32[64,2048]{1,0:T(8,128)}, u32[]{:S(2)}) copy-start(f32[64,2048]{1,0:T(8,128)} %param.13) | copy-start | bytes 1572868
  7.2 29.2 %copy-start.10 = (f32[64,2048]{1,0:T(8,128)S(1)}, f32[64,2048]{1,0:T(8,128)}, u32[]{:S(2)}) copy-start(f32[64,2048]{1,0:T(8,128)} %param.11) | copy-start | bytes 1572868
  7.2 36.2 %copy-start.15 = (f32[1024]{0:T(1024)S(1)}, f32[1024]{0:T(1024)}, u32[]{:S(2)}) copy-start(f32[1024]{0:T(1024)} %param.17) | copy-start | bytes 12292
  7.2 29.2 %reduce-scatter.10.cloned.1.call-start = ((), (), s32[]{:S(2)}) async-start(), calls=%async_computation.9 | async-start | bytes 655360 | tf_op jit(solution)/shard_map/reduce_scatter | solution.py:34
  11.9 58.7 %reduce-scatter.12.cloned.1.call-start = ((), (), s32[]{:S(2)}) async-start(), calls=%async_computation.10 | async-start | bytes 655360 | tf_op jit(solution)/shard_map/reduce_scatter | solution.py:34
  36.5 10.1 %copy-start = (bf16[2048,1024]{1,0:T(8,128)(2,1)S(1)}, bf16[2048,1024]{1,0:T(8,128)(2,1)}, u32[]{:S(2)}) copy-start(bf16[2048,1024]{1,0:T(8,128)(2,1)} %param.10) | copy-start | bytes 12582916
  48.8 56.0 %reduce-scatter.14.cloned.1.call-start = ((), (), s32[]{:S(2)}) async-start(), calls=%async_computation.11 | async-start | bytes 655360 | tf_op jit(solution)/shard_map/reduce_scatter | solution.py:34
  70.6 10.1 %copy-start.1 = (bf16[2048,1024]{1,0:T(8,128)(2,1)S(1)}, bf16[2048,1024]{1,0:T(8,128)(2,1)}, u32[]{:S(2)}) copy-start(bf16[2048,1024]{1,0:T(8,128)(2,1)} %param.10) | copy-start | bytes 12582916
  83.0 56.0 %reduce-scatter.16.cloned.1.call-start = ((), (), s32[]{:S(2)}) async-start(), calls=%async_computation.12 | async-start | bytes 655360 | tf_op jit(solution)/shard_map/reduce_scatter | solution.py:34
  104.8 10.1 %copy-start.2 = (bf16[2048,1024]{1,0:T(8,128)(2,1)S(1)}, bf16[2048,1024]{1,0:T(8,128)(2,1)}, u32[]{:S(2)}) copy-start(bf16[2048,1024]{1,0:T(8,128)(2,1)} %param.10) | copy-start | bytes 12582916
  117.1 56.0 %reduce-scatter.18.cloned.1.call-start = ((), (), s32[]{:S(2)}) async-start(), calls=%async_computation.13 | async-start | bytes 655360 | tf_op jit(solution)/shard_map/reduce_scatter | solution.py:34
  139.0 10.1 %copy-start.3 = (bf16[2048,1024]{1,0:T(8,128)(2,1)S(1)}, bf16[2048,1024]{1,0:T(8,128)(2,1)}, u32[]{:S(2)}) copy-start(bf16[2048,1024]{1,0:T(8,128)(2,1)} %param.10) | copy-start | bytes 12582916
  151.3 56.0 %reduce-scatter.20.cloned.1.call-start = ((), (), s32[]{:S(2)}) async-start(), calls=%async_computation.14 | async-start | bytes 655360 | tf_op jit(solution)/shard_map/reduce_scatter | solution.py:34
  173.1 10.1 %copy-start.4 = (bf16[2048,1024]{1,0:T(8,128)(2,1)S(1)}, bf16[2048,1024]{1,0:T(8,128)(2,1)}, u32[]{:S(2)}) copy-start(bf16[2048,1024]{1,0:T(8,128)(2,1)} %param.10) | copy-start | bytes 12582916
  185.4 56.0 %reduce-scatter.22.cloned.1.call-start = ((), (), s32[]{:S(2)}) async-start(), calls=%async_computation.15 | async-start | bytes 655360 | tf_op jit(solution)/shard_map/reduce_scatter | solution.py:34
  207.3 10.1 %copy-start.5 = (bf16[2048,1024]{1,0:T(8,128)(2,1)S(1)}, bf16[2048,1024]{1,0:T(8,128)(2,1)}, u32[]{:S(2)}) copy-start(bf16[2048,1024]{1,0:T(8,128)(2,1)} %param.10) | copy-start | bytes 12582916
  219.6 56.0 %reduce-scatter.24.cloned.1.call-start = ((), (), s32[]{:S(2)}) async-start(), calls=%async_computation.16 | async-start | bytes 655360 | tf_op jit(solution)/shard_map/reduce_scatter | solution.py:34
  241.4 10.1 %copy-start.6 = (bf16[2048,1024]{1,0:T(8,128)(2,1)S(1)}, bf16[2048,1024]{1,0:T(8,128)(2,1)}, u32[]{:S(2)}) copy-start(bf16[2048,1024]{1,0:T(8,128)(2,1)} %param.10) | copy-start | bytes 12582916
  251.5 31.1 %copy-start.18 = (f32[64]{0:T(128)S(1)}, f32[64]{0:T(128)}, u32[]{:S(2)}) copy-start(f32[64]{0:T(128)} %param.19) | copy-start | bytes 772
  253.8 99.4 %reduce-scatter.26.cloned.1.call-start = ((), (), s32[]{:S(2)}) async-start(), calls=%async_computation.17 | async-start | bytes 655360 | tf_op jit(solution)/shard_map/reduce_scatter | solution.py:48
  275.6 10.2 %copy-start.7 = (bf16[2048,1024]{1,0:T(8,128)(2,1)S(1)}, bf16[2048,1024]{1,0:T(8,128)(2,1)}, u32[]{:S(2)}) copy-start(bf16[2048,1024]{1,0:T(8,128)(2,1)} %param.10) | copy-start | bytes 12582916
  285.7 69.0 %copy-start.11 = (f32[64,1024]{1,0:T(8,128)}, f32[64,1024]{1,0:T(8,128)S(1)}, u32[]{:S(2)}) copy-start(f32[64,1024]{1,0:T(8,128)S(1)} %get-tuple-element.15) | copy-start | bytes 786436
  312.0 42.7 %copy-start.17 = (f32[1024]{0:T(1024)}, f32[1024]{0:T(1024)S(1)}, u32[]{:S(2)}) copy-start(f32[1024]{0:T(1024)S(1)} %get-tuple-element.11) | copy-start | bytes 12292
Sparse Core Ops, SparseCore 0:
  12.0 24.3 reduce-scatter.9
  48.9 21.6 reduce-scatter.11
  83.1 21.6 reduce-scatter.13
  117.2 21.6 reduce-scatter.15
  151.4 21.6 reduce-scatter.17
  185.5 21.6 reduce-scatter.19
  219.7 21.6 reduce-scatter.21
  253.9 21.6 reduce-scatter.23
  288.1 21.6 reduce-scatter.25
where the time goes:
time: 365 us; the launch traced here: 364 us
  waiting for transfers between devices  177 us (48%)
  blocking collectives  107 us (29%)
  matrix products  46.9 us (13%)
  between operations  19.1 us (5%)
  other arithmetic  13.6 us (4%)
    reduce_scatter x8, waiting for transfers between devices, per_device(): lax.psum_scatter(partial_value, 'blk', scatter_dimension=1, tiled=True)  177 us
    all_gather x8, blocking collectives, per_device(): lax.all_gather(weighted_share, 'blk', axis=1, tiled=True)  47.3 us
    psum x1, blocking collectives, per_device(): primal_sum, dual_sum = lax.psum((primal_local, dual_local), ('scen', 'blk'))  37 us
    dot_general x8, matrix products, per_device(): jnp.dot(lax.all_gather(weighted_share, 'blk', axis=1, tiled=True), cons_m...  24.7 us
    psum x1, blocking collectives, per_device(): sums, total = lax.psum((local_sum, local_total), 'scen')  22.2 us
    dot_general x9, matrix products, per_device(): lax.dot_general(x_now.astype(jnp.bfloat16), cons_matrix, contract, prefer...  22.2 us
    convert_element_type x8, other arithmetic, per_device(): weighted_share = (own_scale * (own_mult + aug_weight * (own_scale * prod_...  8.73 us
  transfers between devices with their start and end apart: 9, of which 8 were waited for; matrix products, arithmetic and copies ran while one was open for 1% of the time, Pallas kernels for 0%

commit v1 on v0

v1 whole, which is shorter than its diff:
```python
import functools

import jax
import jax.numpy as jnp
from jax import lax
from jax.experimental import pallas as pl
from jax.experimental.pallas import tpu as pltpu
from jax.sharding import PartitionSpec as P

ITERS = 8
MESH = pl.DeviceIdType.MESH

penalty = 1.0
aug_weight = 1.0
step_size = 0.05
eps = 1e-06


def kernel(
    n_blk, n_scen,
    a, row_scale, rhs, mult, cost, ph, start, consensus, upper, prob,
    sol_out, mult_out, z_out, w_out, primal_out, dual_out,
    a_v, at_v, scale_v, rhs_v, mult_v, sq_v, lin_v, cost_v, ph_v, ph_far, x_v, xb_v, base_v,
    cons_v, up_v, prob_v, p_v, acc_v, send_v, recv_v, end_v, x_far, m_send, m_far, sums_v, norms_v,
    local_sem, pair_send, pair_recv, y_send, y_recv, end_send, end_recv, s_send, s_recv, n_send, n_recv,
):
    n_red = n_blk // 2
    n_chunk, rows, nv = a_v.shape[1:]
    half = x_v.shape[1]
    b, s = lax.axis_index("blk"), lax.axis_index("scen")
    group, core = lax.div(b, 2), lax.rem(b, 2)
    partner = {"blk": b + 1 - 2 * core}
    own_rows = pl.ds(pl.multiple_of(core * half, half), half)
    far_rows = pl.ds(pl.multiple_of((1 - core) * half, half), half)

    def peer(j):
        return {"blk": lax.rem(group + j, n_red) * 2 + core}

    def scen_peer(j):
        return {"scen": lax.rem(s + j, n_scen)}

    def blk_peer(j):
        return {"blk": lax.rem(b + j, n_blk)}

    def remote(src, dst, send, recv, device):
        return pltpu.make_async_remote_copy(
            src_ref=src, dst_ref=dst, send_sem=send, recv_sem=recv, device_id=device, device_id_type=MESH
        )

    barrier = pltpu.get_barrier_semaphore()
    for j in range(1, n_blk):
        pl.semaphore_signal(barrier, inc=1, device_id=blk_peer(j), device_id_type=MESH)
    for j in range(1, n_scen):
        pl.semaphore_signal(barrier, inc=1, device_id=scen_peer(j), device_id_type=MESH)

    local = []

    def fetch(src, dst):
        copy = pltpu.make_async_copy(src, dst, local_sem.at[len(local)])
        copy.start()
        local.append(copy)

    for k in range(n_chunk):
        fetch(a.at[pl.ds(k * rows, rows), :], a_v.at[0, k])
    fetch(row_scale.at[own_rows, :], scale_v)
    fetch(rhs.at[own_rows, :], rhs_v)
    fetch(mult.at[own_rows, :], mult_v)
    fetch(cost.at[own_rows, :], cost_v.at[0])
    fetch(start.at[own_rows, :], x_v.at[0])
    fetch(ph, ph_v)
    fetch(consensus, cons_v.at[0])
    fetch(upper, up_v.at[0])
    fetch(prob, prob_v)

    pl.semaphore_wait(barrier, n_blk + n_scen - 2)

    pair = []

    def push(src, dst):
        n = len(pair)
        copy = remote(src, dst, pair_send.at[n], pair_recv.at[n], partner)
        copy.start()
        pair.append(copy)

    push(cost.at[far_rows, :], cost_v.at[1])
    push(ph.at[far_rows, :], ph_far)
    push(start.at[far_rows, :], x_v.at[1])
    push(consensus, cons_v.at[1])
    push(upper, up_v.at[1])
    for k in range(n_chunk):
        push(a.at[pl.ds(k * rows, rows), :], a_v.at[1, k])

    for k in range(n_chunk):
        local[k].wait()
        at_v[k, 0] = a_v[0, k].T
    for copy in local[n_chunk:]:
        copy.wait()
    for k in range(n_chunk):
        lanes = pl.ds(k * rows, rows)
        scale = scale_v[:, lanes]
        sq_v[k] = aug_weight * scale * scale
        lin_v[k] = scale * (mult_v[:, lanes] - aug_weight * rhs_v[:, lanes])
    base_v[0] = cost_v[0] + ph_v[own_rows, :] - penalty * cons_v[0]
    for copy in pair[:5]:
        copy.wait()
    base_v[1] = cost_v[1] + ph_far[...] - penalty * cons_v[1]
    xb_v[...] = x_v[...].astype(jnp.bfloat16)
    for k in range(n_chunk):
        pair[5 + k].wait()
        at_v[k, 1] = a_v[1, k].T

    def product(k):
        return jnp.dot(xb_v[0], at_v[k, 0], preferred_element_type=jnp.float32) + jnp.dot(
            xb_v[1], at_v[k, 1], preferred_element_type=jnp.float32
        )

    def step(t, carry):
        slot = lax.rem(t, 2)
        copies = []
        for k in range(n_chunk):
            p = product(k)
            p_v[k] = p
            send_v[slot, k] = p.astype(jnp.bfloat16)
            row = []
            for j in range(1, n_red):
                copy = remote(
                    send_v.at[slot, k], recv_v.at[slot, j - 1, k],
                    y_send.at[slot, j - 1, k], y_recv.at[slot, j - 1, k], peer(j),
                )
                copy.start()
                row.append(copy)
            copies.append(row)
        for k in range(n_chunk):
            total = p_v[k]
            for j in range(1, n_red):
                copies[k][j - 1].wait_recv()
                total = total + recv_v[slot, j - 1, k].astype(jnp.float32)
            weighted = (lin_v[k] + sq_v[k] * total).astype(jnp.bfloat16)
            for i in range(2):
                back = jnp.dot(weighted, a_v[i, k], preferred_element_type=jnp.float32)
                acc_v[i] = back if k == 0 else acc_v[i] + back
        for i in range(2):
            x = x_v[i]
            grad = base_v[i] + penalty * x + acc_v[i]
            box = up_v[i]
            x = jnp.clip(x - step_size * grad, -box, box)
            x_v[i] = x
            xb_v[i] = x.astype(jnp.bfloat16)
        for row in copies:
            for copy in row:
                copy.wait_send()
        return carry

    lax.fori_loop(0, ITERS, step, 0)

    n = len(pair)
    push(x_v.at[1], x_far)

    ends = []
    for j in range(1, n_red):
        other = lax.rem(group + j, n_red) * 2
        for i in range(2):
            p_v[other + i] = product(other + i)
            copy = remote(
                p_v.at[other + i], end_v.at[j - 1, i], end_send.at[j - 1, i], end_recv.at[j - 1, i], peer(j)
            )
            copy.start()
            ends.append(copy)

    square = prob_v.shape[1]
    diagonal = lax.broadcasted_iota(jnp.int32, (square, square), 0) == lax.broadcasted_iota(
        jnp.int32, (square, square), 1
    )
    prob_col = jnp.sum(jnp.where(diagonal, prob_v[...], 0.0), axis=1, keepdims=True)
    part_total = jnp.sum(prob_col, axis=0, keepdims=True)
    sol_out[own_rows, :] = x_v[0]
    pair[n].wait()
    sol_out[far_rows, :] = x_far[...]
    x_end = sol_out[...]
    part_sum = jnp.sum(prob_col * x_end, axis=0, keepdims=True)
    spread = jnp.sum(prob_col * (x_end - part_sum / part_total) ** 2, axis=0, keepdims=True)
    spread = jnp.sum(spread, axis=1, keepdims=True)
    sums_v[s, :, pl.ds(0, nv)] = part_sum
    sums_v[s, :, pl.ds(nv, 128)] = jnp.broadcast_to(part_total, (1, 128))
    sums_v[s, :, pl.ds(nv + 128, 128)] = jnp.broadcast_to(spread, (1, 128))
    gathers = []
    for j in range(1, n_scen):
        copy = remote(sums_v.at[s], sums_v.at[s], s_send.at[j - 1], s_recv.at[j - 1], scen_peer(j))
        copy.start()
        gathers.append(copy)

    for i in range(2):
        p_v[group * 2 + i] = product(group * 2 + i)
    for copy in ends:
        copy.wait()

    def new_mult(i):
        k = group * 2 + i
        total = p_v[k]
        for j in range(1, n_red):
            total = total + end_v[j - 1, i]
        lanes = pl.ds(pl.multiple_of(k * rows, rows), rows)
        return mult_v[:, lanes] + aug_weight * (scale_v[:, lanes] * total - rhs_v[:, lanes])

    m_send[...] = new_mult(1 - core)
    n = len(pair)
    push(m_send, m_far)
    mult_out[own_rows, :] = new_mult(core)

    for copy in gathers:
        copy.wait()
    total_sum = sums_v[0, :, pl.ds(0, nv)]
    total = sums_v[0, :, pl.ds(nv, 128)]
    primal = sums_v[0, :, pl.ds(nv + 128, 128)]
    for i in range(1, n_scen):
        total_sum = total_sum + sums_v[i, :, pl.ds(0, nv)]
        total = total + sums_v[i, :, pl.ds(nv, 128)]
        primal = primal + sums_v[i, :, pl.ds(nv + 128, 128)]
    z_new = total_sum / total[:, :1]
    between = jnp.zeros_like(z_new)
    for i in range(n_scen):
        weight = sums_v[i, :, pl.ds(nv, 128)][:, :1]
        between = between + weight * (sums_v[i, :, pl.ds(0, nv)] / weight - z_new) ** 2
    primal = primal + jnp.sum(between, axis=1, keepdims=True)
    dual = jnp.sum((z_new - cons_v[0]) ** 2, axis=1, keepdims=True)
    norms_v[b, :, pl.ds(0, 128)] = primal
    norms_v[b, :, pl.ds(128, 128)] = jnp.broadcast_to(dual, (1, 128))
    norms = []
    for j in range(1, n_blk):
        copy = remote(norms_v.at[b], norms_v.at[b], n_send.at[j - 1], n_recv.at[j - 1], blk_peer(j))
        copy.start()
        norms.append(copy)
    z_out[...] = z_new
    w_out[...] = ph_v[...] + penalty * (sol_out[...] - z_new)
    pair[n].wait()
    mult_out[far_rows, :] = m_far[...]
    for copy in norms:
        copy.wait()
    primal = norms_v[0, :, pl.ds(0, 128)]
    dual = norms_v[0, :, pl.ds(128, 128)]
    for i in range(1, n_blk):
        primal = primal + norms_v[i, :, pl.ds(0, 128)]
        dual = dual + norms_v[i, :, pl.ds(128, 128)]
    width = nv * n_blk
    primal_out[...] = jnp.sqrt(primal / (total * width) + eps)
    dual_out[...] = penalty * jnp.sqrt(dual / width + eps)


def solution(mesh):
    n_blk, n_scen = mesh.shape["blk"], mesh.shape["scen"]
    f32, bf16 = jnp.float32, jnp.bfloat16

    def per_device(cons_matrix, row_scale, rhs, cons_mult, cost, ph_mult, start, consensus, upper, prob):
        m, nv = cons_matrix.shape
        scen = cost.shape[0]
        half, rows = scen // 2, m // n_blk
        n_red = n_blk // 2
        any_spec = pl.BlockSpec(memory_space=pl.ANY)
        vmem = pl.BlockSpec(memory_space=pltpu.VMEM)
        dma = pltpu.SemaphoreType.DMA
        sol, mult_new, z_new, w_new, primal, dual = pl.pallas_call(
            functools.partial(kernel, n_blk, n_scen),
            out_shape=(
                jax.ShapeDtypeStruct((scen, nv), f32),
                jax.ShapeDtypeStruct((scen, rows), f32),
                jax.ShapeDtypeStruct((1, nv), f32),
                jax.ShapeDtypeStruct((scen, nv), f32),
                jax.ShapeDtypeStruct((1, 128), f32),
                jax.ShapeDtypeStruct((1, 128), f32),
            ),
            in_specs=[any_spec] * 10,
            out_specs=[vmem] * 6,
            scratch_shapes=[
                pltpu.VMEM((2, n_blk, rows, nv), bf16),
                pltpu.VMEM((n_blk, 2, nv, rows), bf16),
                pltpu.VMEM((half, m), f32),
                pltpu.VMEM((half, m), f32),
                pltpu.VMEM((half, m), f32),
                pltpu.VMEM((n_blk, half, rows), f32),
                pltpu.VMEM((n_blk, half, rows), f32),
                pltpu.VMEM((2, half, nv), f32),
                pltpu.VMEM((scen, nv), f32),
                pltpu.VMEM((half, nv), f32),
                pltpu.VMEM((2, half, nv), f32),
                pltpu.VMEM((2, half, nv), bf16),
                pltpu.VMEM((2, half, nv), f32),
                pltpu.VMEM((2, 1, nv), f32),
                pltpu.VMEM((2, 1, nv), f32),
                pltpu.VMEM((1, scen), f32),
                pltpu.VMEM((n_blk, half, rows), f32),
                pltpu.VMEM((2, half, nv), f32),
                pltpu.VMEM((2, n_blk, half, rows), bf16),
                pltpu.VMEM((2, n_red - 1, n_blk, half, rows), bf16),
                pltpu.VMEM((n_red - 1, 2, half, rows), f32),
                pltpu.VMEM((half, nv), f32),
                pltpu.VMEM((half, rows), f32),
                pltpu.VMEM((half, rows), f32),
                pltpu.VMEM((n_scen, 1, nv + 256), f32),
                pltpu.VMEM((n_blk, 1, 256), f32),
                dma((n_blk + 9,)),
                dma((n_blk + 7,)),
                dma((n_blk + 7,)),
                dma((2, n_red - 1, n_blk)),
                dma((2, n_red - 1, n_blk)),
                dma((n_red - 1, 2)),
                dma((n_red - 1, 2)),
                dma((n_scen - 1,)),
                dma((n_scen - 1,)),
                dma((n_blk - 1,)),
                dma((n_blk - 1,)),
            ],
            compiler_params=pltpu.CompilerParams(
                collective_id=0, has_side_effects=True, vmem_limit_bytes=48 * 1024 * 1024
            ),
        )(
            cons_matrix, row_scale, rhs, cons_mult, cost, ph_mult, start,
            consensus[None, :], upper[None, :], prob[None, :],
        )
        return sol, mult_new, z_new[0], w_new, primal[0, 0], dual[0, 0]

    in_specs = (
        P(None, "blk"),
        P("scen", None),
        P("scen", None),
        P("scen", None),
        P("scen", "blk"),
        P("scen", "blk"),
        P("scen", "blk"),
        P("blk"),
        P("blk"),
        P("scen"),
    )
    out_specs = (P("scen", "blk"), P("scen", "blk"), P("blk"), P("scen", "blk"), P(), P())
    return jax.shard_map(per_device, mesh=mesh, in_specs=in_specs, out_specs=out_specs, check_vma=False)
```

time: 365 us -> 80.4 us (0.22)
  waiting for transfers between devices: 177 us -> 0 us
  blocking collectives: 107 us -> 0 us
  Pallas kernels: 0 us -> 66.4 us
  matrix products: 46.9 us -> 0 us
  between operations: 19.1 us -> 2.99 us
  other arithmetic: 13.6 us -> 0 us
  local copies, waits for them, and re-layouts: 0.08 us -> 10.6 us
    reduce_scatter x9 -> x0, waiting for transfers between devices: 177 us -> none  [the longest x8 177 us: per_device(): lax.psum_scatter(partial_value, 'blk', scatter_dimension=1, tiled=True)]
    pallas_call x0 -> x1, Pallas kernels: none -> 66.4 us  [per_device(): pl.pallas_call(functools.partial(kernel, n_blk, n_scen), out_shape=(jax.S...]
    psum x2 -> x0, blocking collectives: 59.3 us -> none  [the longest x1 37 us: per_device(): primal_sum, dual_sum = lax.psum((primal_local, dual_local), ('scen', 'blk'))]
    all_gather x8 -> x0, blocking collectives: 47.3 us -> none  [per_device(): lax.all_gather(weighted_share, 'blk', axis=1, tiled=True)]
    dot_general x17 -> x0, matrix products: 46.9 us -> none  [the longest x8 24.7 us: per_device(): jnp.dot(lax.all_gather(weighted_share, 'blk', axis=1, tiled=True), cons_m...]
    unnamed x38 -> x22, local copies, waits for them, and re-layouts: 0.08 us -> 10.6 us
    convert_element_type x8 -> x0, other arithmetic: 8.73 us -> none  [per_device(): weighted_share = (own_scale * (own_mult + aug_weight * (own_scale * prod_...]
  transfers between devices with their start and end apart: 9 -> 0, of which waited for: 8 -> 0; matrix products, arithmetic and copies ran while one was open for 1% -> 0% of each run, Pallas kernels for 0% -> 0%
where the time goes in v1:
time: 80.4 us; the launch traced here: 80 us
  Pallas kernels  66.4 us (83%)
  local copies, waits for them, and re-layouts  10.6 us (13%)
  between operations  2.99 us (4%)
    pallas_call x1, Pallas kernels, per_device(): pl.pallas_call(functools.partial(kernel, n_blk, n_scen), out_shape=(jax.S...  66.4 us
    unnamed x22, local copies, waits for them, and re-layouts  10.6 us

profile of v1, /device:TPU:0, one launch (start us, length us, event | category | flops | bytes accessed | tf_op | source)
XLA Modules:
  0.0 80.0 jit_solution(11718257518434758894)
XLA Ops:
  0.6 0.0 copy-start
  0.6 1.0 %copy-done = f32[64,2048]{1,0:T(8,128)S(1)} copy-done((f32[64,2048]{1,0:T(8,128)S(1)}, f32[64,2048]{1,0:T(8,128)}, u32[]{:S(2)}) %copy-start) | copy-done | bytes 524312
  1.7 0.0 copy-start.1
  1.7 1.0 %copy-done.1 = f32[64,2048]{1,0:T(8,128)S(1)} copy-done((f32[64,2048]{1,0:T(8,128)S(1)}, f32[64,2048]{1,0:T(8,128)}, u32[]{:S(2)}) %copy-start.1) | copy-done | bytes 524312
  2.7 0.0 copy-start.2
  2.7 1.0 %copy-done.2 = f32[64,2048]{1,0:T(8,128)S(1)} copy-done((f32[64,2048]{1,0:T(8,128)S(1)}, f32[64,2048]{1,0:T(8,128)}, u32[]{:S(2)}) %copy-start.2) | copy-done | bytes 524312
  3.8 0.0 copy-start.3
  3.8 0.9 %copy-done.3 = f32[64,1024]{1,0:T(8,128)S(1)} copy-done((f32[64,1024]{1,0:T(8,128)S(1)}, f32[64,1024]{1,0:T(8,128)}, u32[]{:S(2)}) %copy-start.3) | copy-done | bytes 262168
  4.7 0.0 copy-start.4
  4.7 0.9 %copy-done.4 = f32[64,1024]{1,0:T(8,128)S(1)} copy-done((f32[64,1024]{1,0:T(8,128)S(1)}, f32[64,1024]{1,0:T(8,128)}, u32[]{:S(2)}) %copy-start.4) | copy-done | bytes 262168
  5.7 0.0 copy-start.5
  5.7 0.9 %copy-done.5 = f32[64,1024]{1,0:T(8,128)S(1)} copy-done((f32[64,1024]{1,0:T(8,128)S(1)}, f32[64,1024]{1,0:T(8,128)}, u32[]{:S(2)}) %copy-start.5) | copy-done | bytes 262168
  6.6 0.0 copy-start.6
  6.6 0.7 copy-done.6
  7.3 0.0 copy-start.7
  7.3 0.7 copy-done.7
  8.0 0.0 copy-start.8
  8.0 0.7 copy-done.8
  8.6 66.4 %shard_map.145 = (f32[64,1024]{1,0:T(8,128)S(1)}, f32[64,512]{1,0:T(8,128)S(1)}, f32[1,1024]{1,0:T(1,128)S(1)}, f32[64,1024]{1,0:T(8,128)S(1)}, f32[1,128]{1,0:T(1,128)S(1)}, /*index=5*/f32[1,128]{1,0:T(1,128)S(1)}) custom-call(bf16[2048,1024]{1,0:T(8,128)(2,1)} %a.1, f32[64,2048]{1,0:T(8,128)S(1)} %copy-done, f32[64,2048]{1,0:T(8,128)S(1)} %copy-done.1, ...), custom_call_target="tpu_custom_call" | custom-call | tf_op jit(solution)/shard_map/pallas_call | solution.py:261
  75.0 0.7 copy.22
  75.7 0.7 copy.23
  76.4 0.6 copy.24
  77.0 0.7 copy.25
Async XLA Ops:
  0.6 1.0 %copy-start = (f32[64,2048]{1,0:T(8,128)S(1)}, f32[64,2048]{1,0:T(8,128)}, u32[]{:S(2)}) copy-start(f32[64,2048]{1,0:T(8,128)} %row_scale.1) | copy-start | bytes 1572868
  1.7 1.0 %copy-start.1 = (f32[64,2048]{1,0:T(8,128)S(1)}, f32[64,2048]{1,0:T(8,128)}, u32[]{:S(2)}) copy-start(f32[64,2048]{1,0:T(8,128)} %rhs.1) | copy-start | bytes 1572868
  2.7 1.0 %copy-start.2 = (f32[64,2048]{1,0:T(8,128)S(1)}, f32[64,2048]{1,0:T(8,128)}, u32[]{:S(2)}) copy-start(f32[64,2048]{1,0:T(8,128)} %mult.1) | copy-start | bytes 1572868
  3.8 0.9 %copy-start.3 = (f32[64,1024]{1,0:T(8,128)S(1)}, f32[64,1024]{1,0:T(8,128)}, u32[]{:S(2)}) copy-start(f32[64,1024]{1,0:T(8,128)} %cost.1) | copy-start | bytes 786436
  4.7 0.9 %copy-start.4 = (f32[64,1024]{1,0:T(8,128)S(1)}, f32[64,1024]{1,0:T(8,128)}, u32[]{:S(2)}) copy-start(f32[64,1024]{1,0:T(8,128)} %ph.1) | copy-start | bytes 786436
  5.7 0.9 %copy-start.5 = (f32[64,1024]{1,0:T(8,128)S(1)}, f32[64,1024]{1,0:T(8,128)}, u32[]{:S(2)}) copy-start(f32[64,1024]{1,0:T(8,128)} %start.1) | copy-start | bytes 786436
  6.6 0.7 copy-start.6
  7.3 0.7 copy-start.7
  8.0 0.7 copy-start.8

commit v2 on v1

--- a/solution.py
+++ b/solution.py
@@ -19,7 +19,7 @@
 def kernel(
     n_blk, n_scen,
     a, row_scale, rhs, mult, cost, ph, start, consensus, upper, prob,
-    sol_out, mult_out, z_out, w_out, primal_out, dual_out,
+    sol_out, mult_out, z_out, primal_out, dual_out,
     a_v, at_v, scale_v, rhs_v, mult_v, sq_v, lin_v, cost_v, ph_v, ph_far, x_v, xb_v, base_v,
     cons_v, up_v, prob_v, p_v, acc_v, send_v, recv_v, end_v, x_far, m_send, m_far, sums_v, norms_v,
     local_sem, pair_send, pair_recv, y_send, y_recv, end_send, end_recv, s_send, s_recv, n_send, n_recv,
@@ -231,7 +231,6 @@
         copy.start()
         norms.append(copy)
     z_out[...] = z_new
-    w_out[...] = ph_v[...] + penalty * (sol_out[...] - z_new)
     pair[n].wait()
     mult_out[far_rows, :] = m_far[...]
     for copy in norms:
@@ -246,6 +245,15 @@
     dual_out[...] = penalty * jnp.sqrt(dual / width + eps)
 
 
+def finish(sol, mult, z, primal, dual, ph, sol_out, mult_out, z_out, w_out, primal_out, dual_out):
+    sol_out[...] = sol[...]
+    mult_out[...] = mult[...]
+    z_out[...] = z[...]
+    w_out[...] = ph[...] + penalty * (sol[...] - z[...])
+    primal_out[...] = primal[...]
+    dual_out[...] = dual[...]
+
+
 def solution(mesh):
     n_blk, n_scen = mesh.shape["blk"], mesh.shape["scen"]
     f32, bf16 = jnp.float32, jnp.bfloat16
@@ -258,18 +266,17 @@
         any_spec = pl.BlockSpec(memory_space=pl.ANY)
         vmem = pl.BlockSpec(memory_space=pltpu.VMEM)
         dma = pltpu.SemaphoreType.DMA
-        sol, mult_new, z_new, w_new, primal, dual = pl.pallas_call(
+        ends = pl.pallas_call(
             functools.partial(kernel, n_blk, n_scen),
             out_shape=(
                 jax.ShapeDtypeStruct((scen, nv), f32),
                 jax.ShapeDtypeStruct((scen, rows), f32),
                 jax.ShapeDtypeStruct((1, nv), f32),
-                jax.ShapeDtypeStruct((scen, nv), f32),
                 jax.ShapeDtypeStruct((1, 128), f32),
                 jax.ShapeDtypeStruct((1, 128), f32),
             ),
             in_specs=[any_spec] * 10,
-            out_specs=[vmem] * 6,
+            out_specs=[vmem] * 5,
             scratch_shapes=[
                 pltpu.VMEM((2, n_blk, rows, nv), bf16),
                 pltpu.VMEM((n_blk, 2, nv, rows), bf16),
@@ -310,12 +317,21 @@
                 dma((n_blk - 1,)),
             ],
             compiler_params=pltpu.CompilerParams(
-                collective_id=0, has_side_effects=True, vmem_limit_bytes=48 * 1024 * 1024
+                collective_id=0, has_side_effects=True, vmem_limit_bytes=67043328
             ),
         )(
             cons_matrix, row_scale, rhs, cons_mult, cost, ph_mult, start,
             consensus[None, :], upper[None, :], prob[None, :],
         )
+        sol, mult_new, z_new, w_new, primal, dual = pl.pallas_call(
+            finish,
+            out_shape=tuple(
+                jax.ShapeDtypeStruct(shape, f32)
+                for shape in ((scen, nv), (scen, rows), (1, nv), (scen, nv), (1, 128), (1, 128))
+            ),
+            in_specs=[vmem] * 6,
+            out_specs=[vmem] * 6,
+        )(*ends, ph_mult)
         return sol, mult_new, z_new[0], w_new, primal[0, 0], dual[0, 0]
 
     in_specs = (

time: 80.4 us -> 70.2 us (0.87)
  local copies, waits for them, and re-layouts: 10.6 us -> 0 us
  Pallas kernels: 66.4 us -> 69.4 us
  between operations: 2.99 us -> 0.64 us
    unnamed x22 -> x0, local copies, waits for them, and re-layouts: 10.6 us -> none
    pallas_call x0 -> x1, Pallas kernels: none -> 1.97 us  [per_device(): pl.pallas_call(finish, out_shape=tuple((jax.ShapeDtypeStruct(shape, f32)...]
    pallas_call x1, Pallas kernels: 66.4 us -> 67.4 us  [per_device(): pl.pallas_call(functools.partial(kernel, n_blk, n_scen), out_shape=(jax.S...]
where the time goes in v2:
time: 70.2 us; the launch traced here: 70.1 us
  Pallas kernels  69.4 us (99%)
    pallas_call x1, Pallas kernels, per_device(): pl.pallas_call(functools.partial(kernel, n_blk, n_scen), out_shape=(jax.S...  67.4 us
    pallas_call x1, Pallas kernels, per_device(): pl.pallas_call(finish, out_shape=tuple((jax.ShapeDtypeStruct(shape, f32)...  1.97 us

profile of v2, /device:TPU:0, one launch (start us, length us, event | category | flops | bytes accessed | tf_op | source)
XLA Modules:
  0.0 70.1 jit_solution(6408456474168199053)
XLA Ops:
  0.6 67.4 %shard_map.145 = (f32[64,1024]{1,0:T(8,128)}, f32[64,512]{1,0:T(8,128)}, f32[1,1024]{1,0:T(1,128)}, f32[1,128]{1,0:T(1,128)}, f32[1,128]{1,0:T(1,128)}) custom-call(bf16[2048,1024]{1,0:T(8,128)(2,1)} %a.1, f32[64,2048]{1,0:T(8,128)} %row_scale.1, f32[64,2048]{1,0:T(8,128)} %rhs.1, f32[64,2048]{1,0:T(8,128)} %mult.1, f32[64,1024]{1,0:T(8,128)} %cost.1, ...), custom_call_target="tpu_custom_call" | custom-call | tf_op jit(solution)/shard_map/pallas_call | solution.py:269
  68.1 2.0 %shard_map.146 = (f32[64,1024]{1,0:T(8,128)}, f32[64,512]{1,0:T(8,128)}, f32[1,1024]{1,0:T(1,128)}, f32[64,1024]{1,0:T(8,128)}, f32[1,128]{1,0:T(1,128)}, /*index=5*/f32[1,128]{1,0:T(1,128)}) custom-call(f32[64,1024]{1,0:T(8,128)} %get-tuple-element.17.sol, f32[64,512]{1,0:T(8,128)} %get-tuple-element.18.mult, f32[1,1024]{1,0:T(1,128)} %get-tuple-element.19.z, ...), custom_call_target="tpu_custom_call" | custom-call | tf_op jit(solution)/shard_map/pallas_call | solution.py:326

commit v3 on v2

--- a/solution.py
+++ b/solution.py
@@ -21,7 +21,7 @@
     a, row_scale, rhs, mult, cost, ph, start, consensus, upper, prob,
     sol_out, mult_out, z_out, primal_out, dual_out,
     a_v, at_v, scale_v, rhs_v, mult_v, sq_v, lin_v, cost_v, ph_v, ph_far, x_v, xb_v, base_v,
-    cons_v, up_v, prob_v, p_v, acc_v, send_v, recv_v, end_v, x_far, m_send, m_far, sums_v, norms_v,
+    cons_v, up_v, prob_v, p_v, acc_v, send_v, recv_v, end_v, x_far, m_send, m_far, sums_v, norms_v, start_v, p_far, p_near,
     local_sem, pair_send, pair_recv, y_send, y_recv, end_send, end_recv, s_send, s_recv, n_send, n_recv,
 ):
     n_red = n_blk // 2
@@ -66,11 +66,24 @@
     fetch(rhs.at[own_rows, :], rhs_v)
     fetch(mult.at[own_rows, :], mult_v)
     fetch(cost.at[own_rows, :], cost_v.at[0])
-    fetch(start.at[own_rows, :], x_v.at[0])
+    fetch(start, start_v)
     fetch(ph, ph_v)
     fetch(consensus, cons_v.at[0])
     fetch(upper, up_v.at[0])
     fetch(prob, prob_v)
+
+    for k in range(n_chunk):
+        local[k].wait()
+        at_v[k, 0] = a_v[0, k].T
+    for copy in local[n_chunk:]:
+        copy.wait()
+    x_v[0] = start_v[own_rows, :]
+    start_own = start_v[own_rows, :].astype(jnp.bfloat16)
+    start_far = start_v[far_rows, :].astype(jnp.bfloat16)
+    for k in range(n_chunk):
+        p_far[k] = jnp.dot(start_far, at_v[k, 0], preferred_element_type=jnp.float32)
+    for k in range(n_chunk):
+        p_v[k] = jnp.dot(start_own, at_v[k, 0], preferred_element_type=jnp.float32)
 
     pl.semaphore_wait(barrier, n_blk + n_scen - 2)
 
@@ -82,54 +95,35 @@
         copy.start()
         pair.append(copy)
 
+    for k in range(n_chunk):
+        push(p_far.at[k], p_near.at[k])
+    for k in range(n_chunk):
+        push(a.at[pl.ds(k * rows, rows), :], a_v.at[1, k])
     push(cost.at[far_rows, :], cost_v.at[1])
     push(ph.at[far_rows, :], ph_far)
     push(start.at[far_rows, :], x_v.at[1])
     push(consensus, cons_v.at[1])
     push(upper, up_v.at[1])
-    for k in range(n_chunk):
-        push(a.at[pl.ds(k * rows, rows), :], a_v.at[1, k])
-
-    for k in range(n_chunk):
-        local[k].wait()
-        at_v[k, 0] = a_v[0, k].T
-    for copy in local[n_chunk:]:
-        copy.wait()
-    for k in range(n_chunk):
-        lanes = pl.ds(k * rows, rows)
-        scale = scale_v[:, lanes]
-        sq_v[k] = aug_weight * scale * scale
-        lin_v[k] = scale * (mult_v[:, lanes] - aug_weight * rhs_v[:, lanes])
-    base_v[0] = cost_v[0] + ph_v[own_rows, :] - penalty * cons_v[0]
-    for copy in pair[:5]:
-        copy.wait()
-    base_v[1] = cost_v[1] + ph_far[...] - penalty * cons_v[1]
-    xb_v[...] = x_v[...].astype(jnp.bfloat16)
-    for k in range(n_chunk):
-        pair[5 + k].wait()
-        at_v[k, 1] = a_v[1, k].T
 
     def product(k):
         return jnp.dot(xb_v[0], at_v[k, 0], preferred_element_type=jnp.float32) + jnp.dot(
             xb_v[1], at_v[k, 1], preferred_element_type=jnp.float32
         )
 
-    def step(t, carry):
-        slot = lax.rem(t, 2)
-        copies = []
-        for k in range(n_chunk):
-            p = product(k)
-            p_v[k] = p
-            send_v[slot, k] = p.astype(jnp.bfloat16)
-            row = []
-            for j in range(1, n_red):
-                copy = remote(
-                    send_v.at[slot, k], recv_v.at[slot, j - 1, k],
-                    y_send.at[slot, j - 1, k], y_recv.at[slot, j - 1, k], peer(j),
-                )
-                copy.start()
-                row.append(copy)
-            copies.append(row)
+    def share(slot, k, p):
+        p_v[k] = p
+        send_v[slot, k] = p.astype(jnp.bfloat16)
+        row = []
+        for j in range(1, n_red):
+            copy = remote(
+                send_v.at[slot, k], recv_v.at[slot, j - 1, k],
+                y_send.at[slot, j - 1, k], y_recv.at[slot, j - 1, k], peer(j),
+            )
+            copy.start()
+            row.append(copy)
+        return row
+
+    def advance(slot, copies):
         for k in range(n_chunk):
             total = p_v[k]
             for j in range(1, n_red):
@@ -149,9 +143,31 @@
         for row in copies:
             for copy in row:
                 copy.wait_send()
+
+    def step(t, carry):
+        slot = lax.rem(t, 2)
+        advance(slot, [share(slot, k, product(k)) for k in range(n_chunk)])
         return carry
 
-    lax.fori_loop(0, ITERS, step, 0)
+    copies = []
+    for k in range(n_chunk):
+        pair[k].wait()
+        copies.append(share(0, k, p_v[k] + p_near[k]))
+    for k in range(n_chunk):
+        lanes = pl.ds(k * rows, rows)
+        scale = scale_v[:, lanes]
+        sq_v[k] = aug_weight * scale * scale
+        lin_v[k] = scale * (mult_v[:, lanes] - aug_weight * rhs_v[:, lanes])
+    base_v[0] = cost_v[0] + ph_v[own_rows, :] - penalty * cons_v[0]
+    for k in range(n_chunk):
+        pair[n_chunk + k].wait()
+        at_v[k, 1] = a_v[1, k].T
+    for copy in pair[2 * n_chunk :]:
+        copy.wait()
+    base_v[1] = cost_v[1] + ph_far[...] - penalty * cons_v[1]
+    advance(0, copies)
+
+    lax.fori_loop(1, ITERS, step, 0)
 
     n = len(pair)
     push(x_v.at[1], x_far)
@@ -304,9 +320,12 @@
                 pltpu.VMEM((half, rows), f32),
                 pltpu.VMEM((n_scen, 1, nv + 256), f32),
                 pltpu.VMEM((n_blk, 1, 256), f32),
+                pltpu.VMEM((scen, nv), f32),
+                pltpu.VMEM((n_blk, half, rows), f32),
+                pltpu.VMEM((n_blk, half, rows), f32),
                 dma((n_blk + 9,)),
-                dma((n_blk + 7,)),
-                dma((n_blk + 7,)),
+                dma((2 * n_blk + 7,)),
+                dma((2 * n_blk + 7,)),
                 dma((2, n_red - 1, n_blk)),
                 dma((2, n_red - 1, n_blk)),
                 dma((n_red - 1, 2)),

time: 70.2 us -> 68 us (0.969)
  Pallas kernels: 69.4 us -> 67.2 us
    pallas_call x1, Pallas kernels: 67.4 us -> 65.3 us  [per_device(): pl.pallas_call(functools.partial(kernel, n_blk, n_scen), out_shape=(jax.S...]
where the time goes in v3:
time: 68 us; the launch traced here: 67.9 us
  Pallas kernels  67.2 us (99%)
    pallas_call x1, Pallas kernels, per_device(): pl.pallas_call(functools.partial(kernel, n_blk, n_scen), out_shape=(jax.S...  65.3 us
    pallas_call x1, Pallas kernels, per_device(): pl.pallas_call(finish, out_shape=tuple((jax.ShapeDtypeStruct(shape, f32)...  1.97 us

profile of v3, /device:TPU:0, one launch (start us, length us, event | category | flops | bytes accessed | tf_op | source)
XLA Modules:
  0.0 67.9 jit_solution(12114188717378700591)
XLA Ops:
  0.6 65.3 %shard_map.145 = (f32[64,1024]{1,0:T(8,128)}, f32[64,512]{1,0:T(8,128)}, f32[1,1024]{1,0:T(1,128)}, f32[1,128]{1,0:T(1,128)}, f32[1,128]{1,0:T(1,128)}) custom-call(bf16[2048,1024]{1,0:T(8,128)(2,1)} %a.1, f32[64,2048]{1,0:T(8,128)} %row_scale.1, f32[64,2048]{1,0:T(8,128)} %rhs.1, f32[64,2048]{1,0:T(8,128)} %mult.1, f32[64,1024]{1,0:T(8,128)} %cost.1, ...), custom_call_target="tpu_custom_call" | custom-call | tf_op jit(solution)/shard_map/pallas_call | solution.py:285
  65.9 2.0 %shard_map.146 = (f32[64,1024]{1,0:T(8,128)}, f32[64,512]{1,0:T(8,128)}, f32[1,1024]{1,0:T(1,128)}, f32[64,1024]{1,0:T(8,128)}, f32[1,128]{1,0:T(1,128)}, /*index=5*/f32[1,128]{1,0:T(1,128)}) custom-call(f32[64,1024]{1,0:T(8,128)} %get-tuple-element.17.sol, f32[64,512]{1,0:T(8,128)} %get-tuple-element.18.mult, f32[1,1024]{1,0:T(1,128)} %get-tuple-element.19.z, ...), custom_call_target="tpu_custom_call" | custom-call | tf_op jit(solution)/shard_map/pallas_call | solution.py:345
